TPU v7x, 256 devices: a whole 4x4x8 slice. The times are simulated.
256 devices in a mesh: rep: 64 (over z, x, core), rows: 4 (over y).
Axes of the slice: x: 4, y: 4, z: 8, core: 2. Of those that a mesh axis runs over, the one named last changes fastest.
Arguments:
- pooled_grad: bfloat16 [262144, 2, 128], P(('rep', 'rows')), may hold values from -6 to 6
- slot_source: int32 [256, 4, 1024], P(('rep', 'rows')), may hold values from 0 to 2047, as said below
- slot_target: int32 [256, 4, 1024], P(('rep', 'rows')), may hold values from 0 to 8191, as said below
- slot_count: int32 [256, 4], P(('rep', 'rows')), may hold values from 128 to 1024, as said below
- table_rows: float32 [2, 16384, 128], P(None, 'rows'), may hold values from -1.5 to 1.5
- accum: float32 [2, 16384], P(None, 'rows'), may hold values from 0.01 to 1
Outputs:
- new_rows: float32 [2, 16384, 128], P(None, 'rows')
- new_accum: float32 [2, 16384], P(None, 'rows')
Inputs may be any that keep to these rules, and one draw needn't show every extreme that they name: `slot_source`: entry q encodes a local sample q // 2 and a table q % 2; the table agrees with that of slot_target at the same slot. `slot_target`: entry t encodes a table t // 4096 and a row t % 4096 of the owner's shard; rows repeat across slots and senders. `slot_count`: slots at or past the count carry no lookup; every sender fills all slots to some owner.
All inputs are finite; a program needn't handle non-finite values.
Results may differ from a plain program's by a relative error of at most 0.0003.
Values may be sent and summed in bfloat16 or wider, within the bound.
No kernel may reach another device: no remote copies, remote signals or barrier semaphores. Data moves between devices by JAX's collectives and lax.ppermute only.
A program may use at most 64 MiB of HBM per device.

v0:
```python
import math
import jax
import jax.numpy as jnp
from jax import lax
from jax.sharding import Mesh
from jax.sharding import PartitionSpec as P

REP_ROWS = ("rep_0", "rep_1", "rep_2", "rows")
LEARN_RATE = 0.1
EPSILON = 1e-06


def rows_for(lines, count):
    spare = -len(lines) % count
    return jnp.pad(lines, [(0, spare)] + [(0, 0)] * (lines.ndim - 1))


def copy_for_each(shard, axis):
    count = lax.axis_size(axis)
    return lax.all_to_all(
        jnp.broadcast_to(shard[None], (count, *shard.shape)), axis, 0, 0, tiled=True
    )


def in_order(parts, dim):
    shape = list(parts.shape[1:])
    shape[dim] *= parts.shape[0]
    return jnp.moveaxis(parts, 0, dim).reshape(shape)


def gather_axes(shard, axes, dim):
    far, near = axes
    leading = copy_for_each(shard, far)
    parts = jnp.swapaxes(copy_for_each(leading, near), 0, 1)
    return in_order(parts.reshape(-1, *shard.shape), dim)


def in_blocks(shard, dim, count):
    shape = shard.shape
    parts = shard.reshape(*shape[:dim], count, shape[dim] // count, *shape[dim + 1 :])
    return jnp.moveaxis(parts, dim, 0)


def summed_on_arrival(shard, axis, dim):
    count = lax.axis_size(axis)
    parts = lax.all_to_all(in_blocks(shard, dim, count), axis, 0, 0, tiled=True)
    return jnp.sum(parts, axis=0)


def sum_by_axis(shard, axes, dim):
    far, near = axes
    own = summed_on_arrival(in_blocks(shard, dim, lax.axis_size(far)), near, dim + 1)
    return jnp.sum(lax.all_to_all(own, far, 0, 0, tiled=True), axis=0)


def nested_sum(shard, axes):
    lines = shard.reshape(-1, shard.shape[-1])
    padded = rows_for(lines, lax.axis_size(axes[0]) * lax.axis_size(axes[1]))
    whole = gather_axes(sum_by_axis(padded, axes, 0), axes, 0)
    return lax.slice_in_dim(whole, 0, len(lines)).reshape(shard.shape)


def accumulate(grads, targets, tables, rows_dev):
    feature = grads.shape[-1]
    flat_rows = grads.reshape(-1, feature)
    lookup_keys = targets.reshape(-1)
    row_total = tables * rows_dev
    block_size = math.gcd(row_total, 512)
    block_count = row_total // block_size
    offsets = jnp.arange(block_size, dtype=jnp.int32)

    def row_block(block_index):
        row_base = block_index * block_size
        matches = (lookup_keys[:, None] == row_base + offsets[None, :]).astype(jnp.bfloat16)
        return jnp.einsum("sr,sw->rw", matches, flat_rows, preferred_element_type=jnp.float32)

    blocks = lax.map(row_block, jnp.arange(block_count, dtype=jnp.int32))
    return blocks.reshape(tables, rows_dev, feature)


def pick_rows(flat_grad, lookup_keys):
    slot_total = lookup_keys.shape[0]
    block_size = math.gcd(slot_total, 1024)
    block_count = slot_total // block_size
    sources = jnp.arange(flat_grad.shape[0], dtype=jnp.int32)
    key_blocks = lookup_keys.reshape(block_count, block_size)

    def slot_block(block_keys):
        matches = (block_keys[:, None] == sources[None, :]).astype(jnp.bfloat16)
        return jnp.dot(matches, flat_grad, preferred_element_type=jnp.float32).astype(jnp.bfloat16)

    blocks = lax.map(slot_block, key_blocks)
    return blocks.reshape(slot_total, flat_grad.shape[1])


def adagrad(rows_part, state_part, row_grad):
    updated = state_part + jnp.mean(row_grad * row_grad, axis=2)
    shifted = rows_part - LEARN_RATE * row_grad / (jnp.sqrt(updated)[:, :, None] + EPSILON)
    return (shifted, updated)


def shards(pooled_grad, slot_source, slot_target, slot_count, table_rows, accum):
    tables = pooled_grad.shape[1]
    feature = pooled_grad.shape[2]
    rows_dev = table_rows.shape[1]
    owner_total = slot_source.shape[1]
    slot_total = slot_source.shape[2]
    flat_grad = pooled_grad.reshape(-1, feature)
    source = slot_source[0]
    target = slot_target[0]
    counts = slot_count[0]
    slot_ids = jnp.arange(slot_total, dtype=jnp.int32)
    filled = slot_ids[None, :] < counts[:, None]
    source_keys = jnp.where(filled, source, -1).reshape(-1)
    picked = pick_rows(flat_grad, source_keys).reshape(owner_total, slot_total, feature)
    targets = jnp.where(filled, target, -1)
    got_grads, got_targets = (
        lax.all_to_all(picked, "rows", split_axis=0, concat_axis=0, tiled=True),
        lax.all_to_all(targets, "rows", split_axis=0, concat_axis=0, tiled=True),
    )
    partial_grad = accumulate(got_grads, got_targets, tables, rows_dev)
    row_grad = nested_sum(partial_grad, (("rep_0", "rep_1"), "rep_2"))
    new_rows, new_accum = adagrad(table_rows, accum, row_grad)
    return (new_rows, new_accum)


def solution(mesh):
    split = Mesh(
        mesh.devices.reshape(8, 4, 2, mesh.shape["rows"]), ("rep_0", "rep_1", "rep_2", "rows")
    )
    placed = (
        P(REP_ROWS, None, None),
        P(REP_ROWS, None, None),
        P(REP_ROWS, None, None),
        P(REP_ROWS, None),
        P(None, "rows", None),
        P(None, "rows"),
    )
    return jax.shard_map(
        shards,
        mesh=split,
        in_specs=placed,
        out_specs=(P(None, "rows", None), P(None, "rows")),
        check_vma=False,
    )
```

profile of v0, /device:TPU:1, one launch (start us, length us, event | category | flops | bytes accessed | tf_op | source)
XLA Modules:
  0.0 269.6 jit_solution(3844847864048092937)
XLA Ops:
  0.6 1.4 compare_select_fusion
  2.0 5.0 %all-to-all-start = ((s32[4,1,1024]{2,1,0:T(1,128)}), s32[4,1,1024]{2,1,0:T(1,128)S(1)}, u32[]{:S(2)}, u32[]{:S(2)}) async-start(s32[4,1,1024]{2,1,0:T(1,128)} %compare_select_fusion), calls=%async_computation | async-start | bytes 32768 | tf_op jit(solution)/shard_map/all_to_all | solution.py:119
  7.0 0.8 bitcast_select_fusion
  7.8 12.9 %while.22 = (s32[]{:T(128)}, bf16[4,1024,128]{2,1,0:T(8,128)(2,1)}, s32[4,1024]{1,0:T(4,128)S(1)}, bf16[2048,128]{1,0:T(8,128)(2,1)}, s32[]{:T(128)}) while((s32[]{:T(128)}, bf16[4,1024,128]{2,1,0:T(8,128)(2,1)}, s32[4,1024]{1,0:T(4,128)S(1)}, bf16[2048,128]{1,0:T(8,128)(2,1)}, s32[]{:T(128)}) %tuple.50), condition=%wide.region_1.2_spmd.clone, body=%wide.region_0.1_spmd.clone.sunk | while | flops 539099136 | bytes 799297 | solution.py:92
  7.8 3.2 %fusion.27 = bf16[4,1024,128]{2,1,0:T(8,128)(2,1)} fusion(bf16[4,1024,128]{2,1,0:T(8,128)(2,1)} %get-tuple-element.167, s32[]{:T(128)} %get-tuple-element.166, bf16[2048,128]{1,0:T(8,128)(2,1)} %get-tuple-element.174, s32[1024]{0:T(1024)S(1)} %bitcast.54), kind=kOutput, calls=%fused_computation.7.clone.1 | convolution fusion | flops 539099136 | bytes 791040 | tf_op jit(solution)/shard_map/while/body/eval_jaxpr/dot_general | solution.py:90
  11.1 3.2 %fusion.27 = bf16[4,1024,128]{2,1,0:T(8,128)(2,1)} fusion(bf16[4,1024,128]{2,1,0:T(8,128)(2,1)} %get-tuple-element.167, s32[]{:T(128)} %get-tuple-element.166, bf16[2048,128]{1,0:T(8,128)(2,1)} %get-tuple-element.174, s32[1024]{0:T(1024)S(1)} %bitcast.54), kind=kOutput, calls=%fused_computation.7.clone.1 | convolution fusion | flops 539099136 | bytes 791040 | tf_op jit(solution)/shard_map/while/body/eval_jaxpr/dot_general | solution.py:90
  14.3 3.2 %fusion.27 = bf16[4,1024,128]{2,1,0:T(8,128)(2,1)} fusion(bf16[4,1024,128]{2,1,0:T(8,128)(2,1)} %get-tuple-element.167, s32[]{:T(128)} %get-tuple-element.166, bf16[2048,128]{1,0:T(8,128)(2,1)} %get-tuple-element.174, s32[1024]{0:T(1024)S(1)} %bitcast.54), kind=kOutput, calls=%fused_computation.7.clone.1 | convolution fusion | flops 539099136 | bytes 791040 | tf_op jit(solution)/shard_map/while/body/eval_jaxpr/dot_general | solution.py:90
  17.5 3.2 %fusion.27 = bf16[4,1024,128]{2,1,0:T(8,128)(2,1)} fusion(bf16[4,1024,128]{2,1,0:T(8,128)(2,1)} %get-tuple-element.167, s32[]{:T(128)} %get-tuple-element.166, bf16[2048,128]{1,0:T(8,128)(2,1)} %get-tuple-element.174, s32[1024]{0:T(1024)S(1)} %bitcast.54), kind=kOutput, calls=%fused_computation.7.clone.1 | convolution fusion | flops 539099136 | bytes 791040 | tf_op jit(solution)/shard_map/while/body/eval_jaxpr/dot_general | solution.py:90
  20.7 4.2 %all-to-all-start.1 = ((bf16[4,1024,128]{2,1,0:T(8,128)(2,1)}), bf16[4,1024,128]{2,1,0:T(8,128)(2,1)S(1)}, u32[]{:S(2)}, u32[]{:S(2)}) async-start(bf16[4,1024,128]{2,1,0:T(8,128)(2,1)} %get-tuple-element.61), calls=%async_computation.1 | async-start | bytes 2097152 | tf_op jit(solution)/shard_map/all_to_all | solution.py:118
  25.0 13.2 %all-to-all-done.1 = bf16[4,1024,128]{2,1,0:T(8,128)(2,1)S(1)} async-done(((bf16[4,1024,128]{2,1,0:T(8,128)(2,1)}), bf16[4,1024,128]{2,1,0:T(8,128)(2,1)S(1)}, u32[]{:S(2)}, u32[]{:S(2)}) %all-to-all-start.1) | async-done | bytes 1048608 | tf_op jit(solution)/shard_map/all_to_all | solution.py:118
  38.2 78.5 %while.23 = (s32[]{:T(128)}, f32[16,512,128]{2,1,0:T(8,128)}, s32[4,1024]{1,0:T(4,128)S(1)}, s32[16]{0:T(128)S(1)}, bf16[4096,128]{1,0:T(8,128)(2,1)S(1)}, /*index=5*/s32[]{:T(128)}, s32[1]{0:T(128)}) while((s32[]{:T(128)}, f32[16,512,128]{2,1,0:T(8,128)}, s32[4,1024]{1,0:T(4,128)S(1)}, s32[16]{0:T(128)S(1)}, ...), condition=%wide.region_3.4_spmd.clone, body=%wide.region_2.3_spmd.clone.sunk | while | flops 538968576 | bytes 1364585 | solution.py:77
  38.2 0.6 dynamic_slice.14
  39.4 3.7 %fusion.30 = f32[16,512,128]{2,1,0:T(8,128)} fusion(f32[16,512,128]{2,1,0:T(8,128)} %get-tuple-element.184, s32[]{:T(128)} %get-tuple-element.183, bf16[4096,128]{1,0:T(8,128)(2,1)S(1)} %get-tuple-element.194, s32[512]{0:T(512)S(1)} %iota_add_fusion.2, s32[4096]{0:T(1024)S(1)} %bitcast.53), kind=kOutput, calls=%fused_computation.14.clone.1 | convolution fusion | flops 538968064 | bytes 1329664 | tf_op jit(solution)/shard_map/while/body/eval_jaxpr/sr,sw->rw/dot_general | solution.py:75
  43.1 0.6 dynamic_slice.14
  44.3 3.7 %fusion.30 = f32[16,512,128]{2,1,0:T(8,128)} fusion(f32[16,512,128]{2,1,0:T(8,128)} %get-tuple-element.184, s32[]{:T(128)} %get-tuple-element.183, bf16[4096,128]{1,0:T(8,128)(2,1)S(1)} %get-tuple-element.194, s32[512]{0:T(512)S(1)} %iota_add_fusion.2, s32[4096]{0:T(1024)S(1)} %bitcast.53), kind=kOutput, calls=%fused_computation.14.clone.1 | convolution fusion | flops 538968064 | bytes 1329664 | tf_op jit(solution)/shard_map/while/body/eval_jaxpr/sr,sw->rw/dot_general | solution.py:75
  48.0 0.6 dynamic_slice.14
  49.3 3.7 %fusion.30 = f32[16,512,128]{2,1,0:T(8,128)} fusion(f32[16,512,128]{2,1,0:T(8,128)} %get-tuple-element.184, s32[]{:T(128)} %get-tuple-element.183, bf16[4096,128]{1,0:T(8,128)(2,1)S(1)} %get-tuple-element.194, s32[512]{0:T(512)S(1)} %iota_add_fusion.2, s32[4096]{0:T(1024)S(1)} %bitcast.53), kind=kOutput, calls=%fused_computation.14.clone.1 | convolution fusion | flops 538968064 | bytes 1329664 | tf_op jit(solution)/shard_map/while/body/eval_jaxpr/sr,sw->rw/dot_general | solution.py:75
  54.2 3.7 %fusion.30 = f32[16,512,128]{2,1,0:T(8,128)} fusion(f32[16,512,128]{2,1,0:T(8,128)} %get-tuple-element.184, s32[]{:T(128)} %get-tuple-element.183, bf16[4096,128]{1,0:T(8,128)(2,1)S(1)} %get-tuple-element.194, s32[512]{0:T(512)S(1)} %iota_add_fusion.2, s32[4096]{0:T(1024)S(1)} %bitcast.53), kind=kOutput, calls=%fused_computation.14.clone.1 | convolution fusion | flops 538968064 | bytes 1329664 | tf_op jit(solution)/shard_map/while/body/eval_jaxpr/sr,sw->rw/dot_general | solution.py:75
  59.1 3.7 %fusion.30 = f32[16,512,128]{2,1,0:T(8,128)} fusion(f32[16,512,128]{2,1,0:T(8,128)} %get-tuple-element.184, s32[]{:T(128)} %get-tuple-element.183, bf16[4096,128]{1,0:T(8,128)(2,1)S(1)} %get-tuple-element.194, s32[512]{0:T(512)S(1)} %iota_add_fusion.2, s32[4096]{0:T(1024)S(1)} %bitcast.53), kind=kOutput, calls=%fused_computation.14.clone.1 | convolution fusion | flops 538968064 | bytes 1329664 | tf_op jit(solution)/shard_map/while/body/eval_jaxpr/sr,sw->rw/dot_general | solution.py:75
  62.7 0.6 dynamic_slice.14
  64.0 3.7 %fusion.30 = f32[16,512,128]{2,1,0:T(8,128)} fusion(f32[16,512,128]{2,1,0:T(8,128)} %get-tuple-element.184, s32[]{:T(128)} %get-tuple-element.183, bf16[4096,128]{1,0:T(8,128)(2,1)S(1)} %get-tuple-element.194, s32[512]{0:T(512)S(1)} %iota_add_fusion.2, s32[4096]{0:T(1024)S(1)} %bitcast.53), kind=kOutput, calls=%fused_computation.14.clone.1 | convolution fusion | flops 538968064 | bytes 1329664 | tf_op jit(solution)/shard_map/while/body/eval_jaxpr/sr,sw->rw/dot_general | solution.py:75
  67.6 0.6 dynamic_slice.14
  68.9 3.7 %fusion.30 = f32[16,512,128]{2,1,0:T(8,128)} fusion(f32[16,512,128]{2,1,0:T(8,128)} %get-tuple-element.184, s32[]{:T(128)} %get-tuple-element.183, bf16[4096,128]{1,0:T(8,128)(2,1)S(1)} %get-tuple-element.194, s32[512]{0:T(512)S(1)} %iota_add_fusion.2, s32[4096]{0:T(1024)S(1)} %bitcast.53), kind=kOutput, calls=%fused_computation.14.clone.1 | convolution fusion | flops 538968064 | bytes 1329664 | tf_op jit(solution)/shard_map/while/body/eval_jaxpr/sr,sw->rw/dot_general | solution.py:75
  72.5 0.6 dynamic_slice.14
  73.8 3.7 %fusion.30 = f32[16,512,128]{2,1,0:T(8,128)} fusion(f32[16,512,128]{2,1,0:T(8,128)} %get-tuple-element.184, s32[]{:T(128)} %get-tuple-element.183, bf16[4096,128]{1,0:T(8,128)(2,1)S(1)} %get-tuple-element.194, s32[512]{0:T(512)S(1)} %iota_add_fusion.2, s32[4096]{0:T(1024)S(1)} %bitcast.53), kind=kOutput, calls=%fused_computation.14.clone.1 | convolution fusion | flops 538968064 | bytes 1329664 | tf_op jit(solution)/shard_map/while/body/eval_jaxpr/sr,sw->rw/dot_general | solution.py:75
  77.5 0.6 dynamic_slice.14
  78.7 3.7 %fusion.30 = f32[16,512,128]{2,1,0:T(8,128)} fusion(f32[16,512,128]{2,1,0:T(8,128)} %get-tuple-element.184, s32[]{:T(128)} %get-tuple-element.183, bf16[4096,128]{1,0:T(8,128)(2,1)S(1)} %get-tuple-element.194, s32[512]{0:T(512)S(1)} %iota_add_fusion.2, s32[4096]{0:T(1024)S(1)} %bitcast.53), kind=kOutput, calls=%fused_computation.14.clone.1 | convolution fusion | flops 538968064 | bytes 1329664 | tf_op jit(solution)/shard_map/while/body/eval_jaxpr/sr,sw->rw/dot_general | solution.py:75
  83.6 3.7 %fusion.30 = f32[16,512,128]{2,1,0:T(8,128)} fusion(f32[16,512,128]{2,1,0:T(8,128)} %get-tuple-element.184, s32[]{:T(128)} %get-tuple-element.183, bf16[4096,128]{1,0:T(8,128)(2,1)S(1)} %get-tuple-element.194, s32[512]{0:T(512)S(1)} %iota_add_fusion.2, s32[4096]{0:T(1024)S(1)} %bitcast.53), kind=kOutput, calls=%fused_computation.14.clone.1 | convolution fusion | flops 538968064 | bytes 1329664 | tf_op jit(solution)/shard_map/while/body/eval_jaxpr/sr,sw->rw/dot_general | solution.py:75
  87.3 0.6 dynamic_slice.14
  88.5 3.7 %fusion.30 = f32[16,512,128]{2,1,0:T(8,128)} fusion(f32[16,512,128]{2,1,0:T(8,128)} %get-tuple-element.184, s32[]{:T(128)} %get-tuple-element.183, bf16[4096,128]{1,0:T(8,128)(2,1)S(1)} %get-tuple-element.194, s32[512]{0:T(512)S(1)} %iota_add_fusion.2, s32[4096]{0:T(1024)S(1)} %bitcast.53), kind=kOutput, calls=%fused_computation.14.clone.1 | convolution fusion | flops 538968064 | bytes 1329664 | tf_op jit(solution)/shard_map/while/body/eval_jaxpr/sr,sw->rw/dot_general | solution.py:75
  93.4 3.7 %fusion.30 = f32[16,512,128]{2,1,0:T(8,128)} fusion(f32[16,512,128]{2,1,0:T(8,128)} %get-tuple-element.184, s32[]{:T(128)} %get-tuple-element.183, bf16[4096,128]{1,0:T(8,128)(2,1)S(1)} %get-tuple-element.194, s32[512]{0:T(512)S(1)} %iota_add_fusion.2, s32[4096]{0:T(1024)S(1)} %bitcast.53), kind=kOutput, calls=%fused_computation.14.clone.1 | convolution fusion | flops 538968064 | bytes 1329664 | tf_op jit(solution)/shard_map/while/body/eval_jaxpr/sr,sw->rw/dot_general | solution.py:75
  98.3 3.7 %fusion.30 = f32[16,512,128]{2,1,0:T(8,128)} fusion(f32[16,512,128]{2,1,0:T(8,128)} %get-tuple-element.184, s32[]{:T(128)} %get-tuple-element.183, bf16[4096,128]{1,0:T(8,128)(2,1)S(1)} %get-tuple-element.194, s32[512]{0:T(512)S(1)} %iota_add_fusion.2, s32[4096]{0:T(1024)S(1)} %bitcast.53), kind=kOutput, calls=%fused_computation.14.clone.1 | convolution fusion | flops 538968064 | bytes 1329664 | tf_op jit(solution)/shard_map/while/body/eval_jaxpr/sr,sw->rw/dot_general | solution.py:75
  103.2 3.7 %fusion.30 = f32[16,512,128]{2,1,0:T(8,128)} fusion(f32[16,512,128]{2,1,0:T(8,128)} %get-tuple-element.184, s32[]{:T(128)} %get-tuple-element.183, bf16[4096,128]{1,0:T(8,128)(2,1)S(1)} %get-tuple-element.194, s32[512]{0:T(512)S(1)} %iota_add_fusion.2, s32[4096]{0:T(1024)S(1)} %bitcast.53), kind=kOutput, calls=%fused_computation.14.clone.1 | convolution fusion | flops 538968064 | bytes 1329664 | tf_op jit(solution)/shard_map/while/body/eval_jaxpr/sr,sw->rw/dot_general | solution.py:75
  108.2 3.7 %fusion.30 = f32[16,512,128]{2,1,0:T(8,128)} fusion(f32[16,512,128]{2,1,0:T(8,128)} %get-tuple-element.184, s32[]{:T(128)} %get-tuple-element.183, bf16[4096,128]{1,0:T(8,128)(2,1)S(1)} %get-tuple-element.194, s32[512]{0:T(512)S(1)} %iota_add_fusion.2, s32[4096]{0:T(1024)S(1)} %bitcast.53), kind=kOutput, calls=%fused_computation.14.clone.1 | convolution fusion | flops 538968064 | bytes 1329664 | tf_op jit(solution)/shard_map/while/body/eval_jaxpr/sr,sw->rw/dot_general | solution.py:75
  113.1 3.7 %fusion.30 = f32[16,512,128]{2,1,0:T(8,128)} fusion(f32[16,512,128]{2,1,0:T(8,128)} %get-tuple-element.184, s32[]{:T(128)} %get-tuple-element.183, bf16[4096,128]{1,0:T(8,128)(2,1)S(1)} %get-tuple-element.194, s32[512]{0:T(512)S(1)} %iota_add_fusion.2, s32[4096]{0:T(1024)S(1)} %bitcast.53), kind=kOutput, calls=%fused_computation.14.clone.1 | convolution fusion | flops 538968064 | bytes 1329664 | tf_op jit(solution)/shard_map/while/body/eval_jaxpr/sr,sw->rw/dot_general | solution.py:75
  116.7 2.5 copy.15
  119.2 10.6 %all_to_all.34 = f32[2,32,128,128]{3,2,1,0:T(8,128)} all-to-all(f32[2,32,128,128]{3,2,1,0:T(8,128)S(1)} %copy.15), channel_id=1, replica_groups=mesh['rep_0'=8,'rep_1'=4,'rep_2'=2,'rows'=4] {'rep_2'}, dimensions={0} | all-to-all | bytes 8388608 | tf_op jit(solution)/shard_map/all_to_all | solution.py:46
  129.8 2.7 %reduce_sum.27 = f32[32,128,128]{2,1,0:T(8,128)S(1)} reduce(f32[2,32,128,128]{3,2,1,0:T(8,128)} %all_to_all.34, f32[]{:T(128)} %constant.22.clone.1), dimensions={0}, to_apply=%region_4.5 | reduce | flops 524288 | bytes 6291460 | tf_op jit(solution)/shard_map/reduce_sum | solution.py:47
  132.5 59.8 %all_to_all.35 = f32[32,128,128]{2,1,0:T(8,128)} all-to-all(f32[32,128,128]{2,1,0:T(8,128)S(1)} %reduce_sum.27), channel_id=1, replica_groups=mesh['rep_0'=8,'rep_1'=4,'rep_2'=2,'rows'=4] {'rep_0','rep_1'}, dimensions={0} | all-to-all | bytes 4194304 | tf_op jit(solution)/shard_map/all_to_all | solution.py:53
  192.3 1.7 reduce_sum.28
  194.2 54.1 %all_to_all.36 = f32[32,128,128]{2,1,0:T(8,128)S(1)} all-to-all(f32[32,128,128]{2,1,0:T(8,128)S(1)} %broadcast_in_dim.42), channel_id=1, replica_groups=mesh['rep_0'=8,'rep_1'=4,'rep_2'=2,'rows'=4] {'rep_0','rep_1'}, dimensions={0} | all-to-all | bytes 4194304 | tf_op jit(solution)/shard_map/all_to_all | solution.py:20
  248.9 10.2 %all_to_all.37 = f32[2,32,128,128]{3,2,1,0:T(8,128)S(1)} all-to-all(f32[2,32,128,128]{3,2,1,0:T(8,128)S(1)} %broadcast_in_dim.43), channel_id=1, replica_groups=mesh['rep_0'=8,'rep_1'=4,'rep_2'=2,'rows'=4] {'rep_2'}, dimensions={0} | all-to-all | bytes 8388608 | tf_op jit(solution)/shard_map/all_to_all | solution.py:20
  259.0 2.0 copy-done
  261.1 1.1 multiply_reduce_fusion
  262.3 0.7 sqrt_add_fusion
  263.0 2.8 %copy_multiply_fusion = f32[2,32,128,128]{3,2,0,1:T(8,128)S(1)} fusion(f32[2,32,128,128]{3,2,1,0:T(8,128)} %copy-done), kind=kLoop, calls=%fused_computation.17 | loop fusion | flops 1048576 | bytes 8388608 | tf_op jit(solution)/shard_map/mul | solution.py:98
  265.7 0.7 copy-done.1
  266.4 3.1 %divide_subtract_fusion = f32[2,4096,128]{2,1,0:T(8,128)} fusion(f32[2,4096,128]{2,1,0:T(8,128)S(1)} %copy-done.1, f32[2,4096,128]{2,1,0:T(8,128)S(1)} %bitcast.48, f32[2,4096]{1,0:T(2,128)S(1)} %get-tuple-element.103), kind=kLoop, calls=%fused_computation.18 | loop fusion | flops 2097152 | bytes 12615680 | tf_op jit(solution)/shard_map/sub | solution.py:98
  (58 shorter events, 5.6 us)
Async XLA Ops:
  2.0 18.7 %all-to-all-start = ((s32[4,1,1024]{2,1,0:T(1,128)}), s32[4,1,1024]{2,1,0:T(1,128)S(1)}, u32[]{:S(2)}, u32[]{:S(2)}) async-start(s32[4,1,1024]{2,1,0:T(1,128)} %compare_select_fusion), calls=%async_computation | async-start | bytes 32768 | tf_op jit(solution)/shard_map/all_to_all | solution.py:119
  20.7 17.4 %all-to-all-start.1 = ((bf16[4,1024,128]{2,1,0:T(8,128)(2,1)}), bf16[4,1024,128]{2,1,0:T(8,128)(2,1)S(1)}, u32[]{:S(2)}, u32[]{:S(2)}) async-start(bf16[4,1024,128]{2,1,0:T(8,128)(2,1)} %get-tuple-element.61), calls=%async_computation.1 | async-start | bytes 2097152 | tf_op jit(solution)/shard_map/all_to_all | solution.py:118
  259.0 2.0 copy-start
  261.1 1.3 copy-start.2
  263.0 3.4 %copy-start.1 = (f32[2,4096,128]{2,1,0:T(8,128)S(1)}, f32[2,4096,128]{2,1,0:T(8,128)}, u32[]{:S(2)}) copy-start(f32[2,4096,128]{2,1,0:T(8,128)} %param.14) | copy-start | bytes 12582916
where the time goes:
time: 270 us
  blocking collectives  135 us (50%)
  matrix products  71.3 us (26%)
  local copies, waits for them, and re-layouts  15.4 us (6%)
  other arithmetic  14.4 us (5%)
  waiting for transfers between devices  13.2 us (5%)
  loops' own time  10.7 us (4%)
  starting transfers between devices  9.24 us (3%)
    all_to_all x2, blocking collectives, copy_for_each(): lax.all_to_all(jnp.broadcast_to(shard[None], (count, *shard.shape)), axis...  64.3 us
    all_to_all x1, blocking collectives, sum_by_axis(): return jnp.sum(lax.all_to_all(own, far, 0, 0, tiled=True), axis=0)  59.8 us
    dot_general x16, matrix products, row_block(): jnp.einsum('sr,sw->rw', matches, flat_rows, preferred_element_type=jnp.fl...  58.4 us
    all_to_all x1, waiting for transfers between devices, shards(): lax.all_to_all(picked, 'rows', split_axis=0, concat_axis=0, tiled=True)  13.2 us
    dot_general x4, matrix products, slot_block(): jnp.dot(matches, flat_grad, preferred_element_type=jnp.float32)  12.9 us
    another operation x1, loops' own time, accumulate(): blocks = lax.map(row_block, jnp.arange(block_count, dtype=jnp.int32))  10.7 us
    all_to_all x1, blocking collectives, summed_on_arrival(): parts = lax.all_to_all(in_blocks(shard, dim, count), axis, 0, 0, tiled=True)  10.6 us
    dynamic_slice x16, local copies, waits for them, and re-layouts, accumulate(): blocks = lax.map(row_block, jnp.arange(block_count, dtype=jnp.int32))  9.32 us
  transfers between devices with their start and end apart: 2, of which 1 were waited for; matrix products, arithmetic and copies ran while one was open for 5% of the time, Pallas kernels for 0%

commit v1 on v0

--- a/solution.py
+++ b/solution.py
@@ -8,6 +8,28 @@
 REP_ROWS = ("rep_0", "rep_1", "rep_2", "rows")
 LEARN_RATE = 0.1
 EPSILON = 1e-06
+
+
+def cut_along(value, dim, devices):
+    before, after = (value.shape[:dim], value.shape[dim + 1 :])
+    return jnp.moveaxis(value.reshape(*before, devices, -1, *after), dim, 0)
+
+
+def in_order_2(pieces, dim):
+    pieces = jnp.moveaxis(pieces, 0, dim)
+    dims = pieces.shape
+    return pieces.reshape(*dims[:dim], dims[dim] * dims[dim + 1], *dims[dim + 2 :])
+
+
+def pairwise_exchange(x, axis, split_dim, concat_dim):
+    length, index = (lax.axis_size(axis), lax.axis_index(axis))
+    tiles = cut_along(x, split_dim, length)
+    outs = [tiles[index]]
+    for hop in range(1, length):
+        sent = tiles[index ^ hop]
+        outs.append(lax.ppermute(sent, axis, [(i, i ^ hop) for i in range(length)]))
+    tiles = jnp.stack(outs)[index ^ jnp.arange(length)]
+    return in_order_2(tiles, concat_dim)
 
 
 def rows_for(lines, count):
@@ -115,7 +137,7 @@
     picked = pick_rows(flat_grad, source_keys).reshape(owner_total, slot_total, feature)
     targets = jnp.where(filled, target, -1)
     got_grads, got_targets = (
-        lax.all_to_all(picked, "rows", split_axis=0, concat_axis=0, tiled=True),
+        pairwise_exchange(picked, "rows", 0, 0),
         lax.all_to_all(targets, "rows", split_axis=0, concat_axis=0, tiled=True),
     )
     partial_grad = accumulate(got_grads, got_targets, tables, rows_dev)

time: 270 us -> 263 us (0.974)
  waiting for transfers between devices: 13.2 us -> 8.98 us
    all_to_all x1 -> x0, waiting for transfers between devices: 13.2 us -> none  [shards(): lax.all_to_all(picked, 'rows', split_axis=0, concat_axis=0, tiled=True)]
    all_to_all x1, waiting for transfers between devices: 0.01 us -> 8.97 us  [shards(): lax.all_to_all(targets, 'rows', split_axis=0, concat_axis=0, tiled=True)]
    ppermute x0 -> x3, starting transfers between devices: none -> 4.82 us  [pairwise_exchange(): outs.append(lax.ppermute(sent, axis, [(i, i ^ hop) for i in range(length)]))]
    all_to_all x1 -> x0, starting transfers between devices: 4.24 us -> none  [shards(): lax.all_to_all(picked, 'rows', split_axis=0, concat_axis=0, tiled=True)]
  transfers between devices with their start and end apart: 2 -> 4, of which waited for: 1 -> 1; matrix products, arithmetic and copies ran while one was open for 5% -> 0% of each run, Pallas kernels for 0% -> 0%
where the time goes in v1:
time: 263 us; the launch traced here: 262 us
  blocking collectives  134 us (51%)
  matrix products  68.9 us (26%)
  local copies, waits for them, and re-layouts  16.2 us (6%)
  other arithmetic  13.8 us (5%)
  loops' own time  10.8 us (4%)
  waiting for transfers between devices  8.98 us (3%)
  starting transfers between devices  8.76 us (3%)
    all_to_all x2, blocking collectives, copy_for_each(): lax.all_to_all(jnp.broadcast_to(shard[None], (count, *shard.shape)), axis...  64.3 us
    all_to_all x1, blocking collectives, sum_by_axis(): return jnp.sum(lax.all_to_all(own, far, 0, 0, tiled=True), axis=0)  59.8 us
    dot_general x16, matrix products, row_block(): jnp.einsum('sr,sw->rw', matches, flat_rows, preferred_element_type=jnp.fl...  58.4 us
    another operation x1, loops' own time, accumulate(): blocks = lax.map(row_block, jnp.arange(block_count, dtype=jnp.int32))  10.7 us
    dot_general x4, matrix products, slot_block(): jnp.dot(matches, flat_grad, preferred_element_type=jnp.float32)  10.5 us
    all_to_all x1, blocking collectives, summed_on_arrival(): parts = lax.all_to_all(in_blocks(shard, dim, count), axis, 0, 0, tiled=True)  9.88 us
    dynamic_slice x16, local copies, waits for them, and re-layouts, accumulate(): blocks = lax.map(row_block, jnp.arange(block_count, dtype=jnp.int32))  9.32 us
    all_to_all x1, waiting for transfers between devices, shards(): lax.all_to_all(targets, 'rows', split_axis=0, concat_axis=0, tiled=True)  8.97 us
  transfers between devices with their start and end apart: 4, of which 1 were waited for; matrix products, arithmetic and copies ran while one was open for 0% of the time, Pallas kernels for 0%

profile of v1, /device:TPU:1, one launch (start us, length us, event | category | flops | bytes accessed | tf_op | source)
XLA Modules:
  0.0 262.2 jit_solution(12685457011015513224)
XLA Ops:
  0.7 0.8 bitcast_select_fusion
  1.5 10.6 %while.22 = (s32[]{:T(128)}, bf16[4,1024,128]{2,1,0:T(8,128)(2,1)S(1)}, s32[4,1024]{1,0:T(4,128)S(1)}, bf16[2048,128]{1,0:T(8,128)(2,1)}, s32[]{:T(128)}) while((s32[]{:T(128)}, bf16[4,1024,128]{2,1,0:T(8,128)(2,1)S(1)}, s32[4,1024]{1,0:T(4,128)S(1)}, bf16[2048,128]{1,0:T(8,128)(2,1)}, s32[]{:T(128)}) %tuple.53), condition=%wide.region_1.2_spmd.clone, body=%wide.region_0.1_spmd.clone.sunk | while | flops 539099136 | bytes 798789 | solution.py:114
  1.5 2.6 %fusion.28 = bf16[4,1024,128]{2,1,0:T(8,128)(2,1)S(1)} fusion(bf16[4,1024,128]{2,1,0:T(8,128)(2,1)S(1)} %get-tuple-element.171, s32[]{:T(128)} %get-tuple-element.170, bf16[2048,128]{1,0:T(8,128)(2,1)} %get-tuple-element.178, s32[1024]{0:T(1024)S(1)} %bitcast.66), kind=kOutput, calls=%fused_computation.8.clone.1 | convolution fusion | flops 539099136 | bytes 790532 | tf_op jit(solution)/shard_map/while/body/eval_jaxpr/dot_general | solution.py:112
  4.1 2.6 fusion.28
  6.8 2.6 fusion.28
  9.4 2.6 fusion.28
  12.2 2.2 collective-permute-start
  14.4 2.6 collective-permute-start.1
  17.0 0.7 compare_select_fusion
  17.7 3.9 %all-to-all-start = ((s32[4,1,1024]{2,1,0:T(1,128)}), s32[4,1,1024]{2,1,0:T(1,128)S(1)}, u32[]{:S(2)}, u32[]{:S(2)}) async-start(s32[4,1,1024]{2,1,0:T(1,128)} %compare_select_fusion), calls=%async_computation | async-start | bytes 32768 | tf_op jit(solution)/shard_map/all_to_all | solution.py:141
  21.6 9.0 %all-to-all-done = s32[4,1,1024]{2,1,0:T(1,128)S(1)} async-done(((s32[4,1,1024]{2,1,0:T(1,128)}), s32[4,1,1024]{2,1,0:T(1,128)S(1)}, u32[]{:S(2)}, u32[]{:S(2)}) %all-to-all-start) | async-done | bytes 16416 | tf_op jit(solution)/shard_map/all_to_all | solution.py:141
  30.8 0.7 gather_fusion
  31.6 78.5 %while.23 = (s32[]{:T(128)}, f32[16,512,128]{2,1,0:T(8,128)}, s32[4,1024]{1,0:T(4,128)S(1)}, s32[16]{0:T(128)S(1)}, bf16[4096,128]{1,0:T(8,128)(2,1)S(1)}, /*index=5*/s32[]{:T(128)}, s32[1]{0:T(128)}) while((s32[]{:T(128)}, f32[16,512,128]{2,1,0:T(8,128)}, s32[4,1024]{1,0:T(4,128)S(1)}, s32[16]{0:T(128)S(1)}, ...), condition=%wide.region_3.4_spmd.clone, body=%wide.region_2.3_spmd.clone.sunk | while | flops 538968576 | bytes 1364585 | solution.py:99
  31.6 0.6 dynamic_slice.21
  32.8 3.7 %fusion.31 = f32[16,512,128]{2,1,0:T(8,128)} fusion(f32[16,512,128]{2,1,0:T(8,128)} %get-tuple-element.188, s32[]{:T(128)} %get-tuple-element.187, bf16[4096,128]{1,0:T(8,128)(2,1)S(1)} %get-tuple-element.198, s32[512]{0:T(512)S(1)} %iota_add_fusion.2, s32[4096]{0:T(1024)S(1)} %bitcast.62), kind=kOutput, calls=%fused_computation.15.clone.1 | convolution fusion | flops 538968064 | bytes 1329664 | tf_op jit(solution)/shard_map/while/body/eval_jaxpr/sr,sw->rw/dot_general | solution.py:97
  36.5 0.6 dynamic_slice.21
  37.7 3.7 %fusion.31 = f32[16,512,128]{2,1,0:T(8,128)} fusion(f32[16,512,128]{2,1,0:T(8,128)} %get-tuple-element.188, s32[]{:T(128)} %get-tuple-element.187, bf16[4096,128]{1,0:T(8,128)(2,1)S(1)} %get-tuple-element.198, s32[512]{0:T(512)S(1)} %iota_add_fusion.2, s32[4096]{0:T(1024)S(1)} %bitcast.62), kind=kOutput, calls=%fused_computation.15.clone.1 | convolution fusion | flops 538968064 | bytes 1329664 | tf_op jit(solution)/shard_map/while/body/eval_jaxpr/sr,sw->rw/dot_general | solution.py:97
  41.4 0.6 dynamic_slice.21
  42.6 3.7 %fusion.31 = f32[16,512,128]{2,1,0:T(8,128)} fusion(f32[16,512,128]{2,1,0:T(8,128)} %get-tuple-element.188, s32[]{:T(128)} %get-tuple-element.187, bf16[4096,128]{1,0:T(8,128)(2,1)S(1)} %get-tuple-element.198, s32[512]{0:T(512)S(1)} %iota_add_fusion.2, s32[4096]{0:T(1024)S(1)} %bitcast.62), kind=kOutput, calls=%fused_computation.15.clone.1 | convolution fusion | flops 538968064 | bytes 1329664 | tf_op jit(solution)/shard_map/while/body/eval_jaxpr/sr,sw->rw/dot_general | solution.py:97
  46.3 0.6 dynamic_slice.21
  47.6 3.7 %fusion.31 = f32[16,512,128]{2,1,0:T(8,128)} fusion(f32[16,512,128]{2,1,0:T(8,128)} %get-tuple-element.188, s32[]{:T(128)} %get-tuple-element.187, bf16[4096,128]{1,0:T(8,128)(2,1)S(1)} %get-tuple-element.198, s32[512]{0:T(512)S(1)} %iota_add_fusion.2, s32[4096]{0:T(1024)S(1)} %bitcast.62), kind=kOutput, calls=%fused_computation.15.clone.1 | convolution fusion | flops 538968064 | bytes 1329664 | tf_op jit(solution)/shard_map/while/body/eval_jaxpr/sr,sw->rw/dot_general | solution.py:97
  51.2 0.6 dynamic_slice.21
  52.5 3.7 %fusion.31 = f32[16,512,128]{2,1,0:T(8,128)} fusion(f32[16,512,128]{2,1,0:T(8,128)} %get-tuple-element.188, s32[]{:T(128)} %get-tuple-element.187, bf16[4096,128]{1,0:T(8,128)(2,1)S(1)} %get-tuple-element.198, s32[512]{0:T(512)S(1)} %iota_add_fusion.2, s32[4096]{0:T(1024)S(1)} %bitcast.62), kind=kOutput, calls=%fused_computation.15.clone.1 | convolution fusion | flops 538968064 | bytes 1329664 | tf_op jit(solution)/shard_map/while/body/eval_jaxpr/sr,sw->rw/dot_general | solution.py:97
  56.1 0.6 dynamic_slice.21
  57.4 3.7 %fusion.31 = f32[16,512,128]{2,1,0:T(8,128)} fusion(f32[16,512,128]{2,1,0:T(8,128)} %get-tuple-element.188, s32[]{:T(128)} %get-tuple-element.187, bf16[4096,128]{1,0:T(8,128)(2,1)S(1)} %get-tuple-element.198, s32[512]{0:T(512)S(1)} %iota_add_fusion.2, s32[4096]{0:T(1024)S(1)} %bitcast.62), kind=kOutput, calls=%fused_computation.15.clone.1 | convolution fusion | flops 538968064 | bytes 1329664 | tf_op jit(solution)/shard_map/while/body/eval_jaxpr/sr,sw->rw/dot_general | solution.py:97
  62.3 3.7 %fusion.31 = f32[16,512,128]{2,1,0:T(8,128)} fusion(f32[16,512,128]{2,1,0:T(8,128)} %get-tuple-element.188, s32[]{:T(128)} %get-tuple-element.187, bf16[4096,128]{1,0:T(8,128)(2,1)S(1)} %get-tuple-element.198, s32[512]{0:T(512)S(1)} %iota_add_fusion.2, s32[4096]{0:T(1024)S(1)} %bitcast.62), kind=kOutput, calls=%fused_computation.15.clone.1 | convolution fusion | flops 538968064 | bytes 1329664 | tf_op jit(solution)/shard_map/while/body/eval_jaxpr/sr,sw->rw/dot_general | solution.py:97
  67.2 3.7 %fusion.31 = f32[16,512,128]{2,1,0:T(8,128)} fusion(f32[16,512,128]{2,1,0:T(8,128)} %get-tuple-element.188, s32[]{:T(128)} %get-tuple-element.187, bf16[4096,128]{1,0:T(8,128)(2,1)S(1)} %get-tuple-element.198, s32[512]{0:T(512)S(1)} %iota_add_fusion.2, s32[4096]{0:T(1024)S(1)} %bitcast.62), kind=kOutput, calls=%fused_computation.15.clone.1 | convolution fusion | flops 538968064 | bytes 1329664 | tf_op jit(solution)/shard_map/while/body/eval_jaxpr/sr,sw->rw/dot_general | solution.py:97
  72.1 3.7 %fusion.31 = f32[16,512,128]{2,1,0:T(8,128)} fusion(f32[16,512,128]{2,1,0:T(8,128)} %get-tuple-element.188, s32[]{:T(128)} %get-tuple-element.187, bf16[4096,128]{1,0:T(8,128)(2,1)S(1)} %get-tuple-element.198, s32[512]{0:T(512)S(1)} %iota_add_fusion.2, s32[4096]{0:T(1024)S(1)} %bitcast.62), kind=kOutput, calls=%fused_computation.15.clone.1 | convolution fusion | flops 538968064 | bytes 1329664 | tf_op jit(solution)/shard_map/while/body/eval_jaxpr/sr,sw->rw/dot_general | solution.py:97
  77.0 3.7 %fusion.31 = f32[16,512,128]{2,1,0:T(8,128)} fusion(f32[16,512,128]{2,1,0:T(8,128)} %get-tuple-element.188, s32[]{:T(128)} %get-tuple-element.187, bf16[4096,128]{1,0:T(8,128)(2,1)S(1)} %get-tuple-element.198, s32[512]{0:T(512)S(1)} %iota_add_fusion.2, s32[4096]{0:T(1024)S(1)} %bitcast.62), kind=kOutput, calls=%fused_computation.15.clone.1 | convolution fusion | flops 538968064 | bytes 1329664 | tf_op jit(solution)/shard_map/while/body/eval_jaxpr/sr,sw->rw/dot_general | solution.py:97
  81.9 3.7 %fusion.31 = f32[16,512,128]{2,1,0:T(8,128)} fusion(f32[16,512,128]{2,1,0:T(8,128)} %get-tuple-element.188, s32[]{:T(128)} %get-tuple-element.187, bf16[4096,128]{1,0:T(8,128)(2,1)S(1)} %get-tuple-element.198, s32[512]{0:T(512)S(1)} %iota_add_fusion.2, s32[4096]{0:T(1024)S(1)} %bitcast.62), kind=kOutput, calls=%fused_computation.15.clone.1 | convolution fusion | flops 538968064 | bytes 1329664 | tf_op jit(solution)/shard_map/while/body/eval_jaxpr/sr,sw->rw/dot_general | solution.py:97
  86.8 3.7 %fusion.31 = f32[16,512,128]{2,1,0:T(8,128)} fusion(f32[16,512,128]{2,1,0:T(8,128)} %get-tuple-element.188, s32[]{:T(128)} %get-tuple-element.187, bf16[4096,128]{1,0:T(8,128)(2,1)S(1)} %get-tuple-element.198, s32[512]{0:T(512)S(1)} %iota_add_fusion.2, s32[4096]{0:T(1024)S(1)} %bitcast.62), kind=kOutput, calls=%fused_computation.15.clone.1 | convolution fusion | flops 538968064 | bytes 1329664 | tf_op jit(solution)/shard_map/while/body/eval_jaxpr/sr,sw->rw/dot_general | solution.py:97
  91.7 3.7 %fusion.31 = f32[16,512,128]{2,1,0:T(8,128)} fusion(f32[16,512,128]{2,1,0:T(8,128)} %get-tuple-element.188, s32[]{:T(128)} %get-tuple-element.187, bf16[4096,128]{1,0:T(8,128)(2,1)S(1)} %get-tuple-element.198, s32[512]{0:T(512)S(1)} %iota_add_fusion.2, s32[4096]{0:T(1024)S(1)} %bitcast.62), kind=kOutput, calls=%fused_computation.15.clone.1 | convolution fusion | flops 538968064 | bytes 1329664 | tf_op jit(solution)/shard_map/while/body/eval_jaxpr/sr,sw->rw/dot_general | solution.py:97
  96.6 3.7 %fusion.31 = f32[16,512,128]{2,1,0:T(8,128)} fusion(f32[16,512,128]{2,1,0:T(8,128)} %get-tuple-element.188, s32[]{:T(128)} %get-tuple-element.187, bf16[4096,128]{1,0:T(8,128)(2,1)S(1)} %get-tuple-element.198, s32[512]{0:T(512)S(1)} %iota_add_fusion.2, s32[4096]{0:T(1024)S(1)} %bitcast.62), kind=kOutput, calls=%fused_computation.15.clone.1 | convolution fusion | flops 538968064 | bytes 1329664 | tf_op jit(solution)/shard_map/while/body/eval_jaxpr/sr,sw->rw/dot_general | solution.py:97
  101.5 3.7 %fusion.31 = f32[16,512,128]{2,1,0:T(8,128)} fusion(f32[16,512,128]{2,1,0:T(8,128)} %get-tuple-element.188, s32[]{:T(128)} %get-tuple-element.187, bf16[4096,128]{1,0:T(8,128)(2,1)S(1)} %get-tuple-element.198, s32[512]{0:T(512)S(1)} %iota_add_fusion.2, s32[4096]{0:T(1024)S(1)} %bitcast.62), kind=kOutput, calls=%fused_computation.15.clone.1 | convolution fusion | flops 538968064 | bytes 1329664 | tf_op jit(solution)/shard_map/while/body/eval_jaxpr/sr,sw->rw/dot_general | solution.py:97
  106.5 3.7 %fusion.31 = f32[16,512,128]{2,1,0:T(8,128)} fusion(f32[16,512,128]{2,1,0:T(8,128)} %get-tuple-element.188, s32[]{:T(128)} %get-tuple-element.187, bf16[4096,128]{1,0:T(8,128)(2,1)S(1)} %get-tuple-element.198, s32[512]{0:T(512)S(1)} %iota_add_fusion.2, s32[4096]{0:T(1024)S(1)} %bitcast.62), kind=kOutput, calls=%fused_computation.15.clone.1 | convolution fusion | flops 538968064 | bytes 1329664 | tf_op jit(solution)/shard_map/while/body/eval_jaxpr/sr,sw->rw/dot_general | solution.py:97
  110.1 2.5 copy.15
  112.6 9.9 %all_to_all.29 = f32[2,32,128,128]{3,2,1,0:T(8,128)} all-to-all(f32[2,32,128,128]{3,2,1,0:T(8,128)S(1)} %copy.15), channel_id=1, replica_groups=mesh['rep_0'=8,'rep_1'=4,'rep_2'=2,'rows'=4] {'rep_2'}, dimensions={0} | all-to-all | bytes 8388608 | tf_op jit(solution)/shard_map/all_to_all | solution.py:68
  122.5 2.7 %reduce_sum.27 = f32[32,128,128]{2,1,0:T(8,128)S(1)} reduce(f32[2,32,128,128]{3,2,1,0:T(8,128)} %all_to_all.29, f32[]{:T(128)} %constant.11.clone.1), dimensions={0}, to_apply=%region_4.5 | reduce | flops 524288 | bytes 6291460 | tf_op jit(solution)/shard_map/reduce_sum | solution.py:69
  125.2 59.8 %all_to_all.30 = f32[32,128,128]{2,1,0:T(8,128)} all-to-all(f32[32,128,128]{2,1,0:T(8,128)S(1)} %reduce_sum.27), channel_id=1, replica_groups=mesh['rep_0'=8,'rep_1'=4,'rep_2'=2,'rows'=4] {'rep_0','rep_1'}, dimensions={0} | all-to-all | bytes 4194304 | tf_op jit(solution)/shard_map/all_to_all | solution.py:75
  184.9 1.7 reduce_sum.28
  186.9 54.1 %all_to_all.31 = f32[32,128,128]{2,1,0:T(8,128)S(1)} all-to-all(f32[32,128,128]{2,1,0:T(8,128)S(1)} %broadcast_in_dim.43), channel_id=1, replica_groups=mesh['rep_0'=8,'rep_1'=4,'rep_2'=2,'rows'=4] {'rep_0','rep_1'}, dimensions={0} | all-to-all | bytes 4194304 | tf_op jit(solution)/shard_map/all_to_all | solution.py:42
  241.5 10.2 %all_to_all.32 = f32[2,32,128,128]{3,2,1,0:T(8,128)S(1)} all-to-all(f32[2,32,128,128]{3,2,1,0:T(8,128)S(1)} %broadcast_in_dim.44), channel_id=1, replica_groups=mesh['rep_0'=8,'rep_1'=4,'rep_2'=2,'rows'=4] {'rep_2'}, dimensions={0} | all-to-all | bytes 8388608 | tf_op jit(solution)/shard_map/all_to_all | solution.py:42
  251.7 2.0 copy-done
  253.7 1.1 multiply_reduce_fusion
  255.0 0.7 sqrt_add_fusion
  255.6 2.8 %copy_multiply_fusion = f32[2,32,128,128]{3,2,0,1:T(8,128)S(1)} fusion(f32[2,32,128,128]{3,2,1,0:T(8,128)} %copy-done), kind=kLoop, calls=%fused_computation.18 | loop fusion | flops 1048576 | bytes 8388608 | tf_op jit(solution)/shard_map/mul | solution.py:120
  258.4 0.7 copy-done.1
  259.1 3.1 %divide_subtract_fusion = f32[2,4096,128]{2,1,0:T(8,128)} fusion(f32[2,4096,128]{2,1,0:T(8,128)S(1)} %copy-done.1, f32[2,4096,128]{2,1,0:T(8,128)S(1)} %bitcast.57, f32[2,4096]{1,0:T(2,128)S(1)} %get-tuple-element.103), kind=kLoop, calls=%fused_computation.19 | loop fusion | flops 2097152 | bytes 12615680 | tf_op jit(solution)/shard_map/sub | solution.py:120
  (71 shorter events, 7.0 us)
Async XLA Ops:
  1.4 15.5 %copy-start.3 = (s32[1,4,1024]{2,1,0:T(4,128)S(1)}, s32[1,4,1024]{2,1,0:T(4,128)}, u32[]{:S(2)}) copy-start(s32[1,4,1024]{2,1,0:T(4,128)} %param.12) | copy-start | bytes 49156
  1.4 15.5 %copy-start.4 = (s32[1,4]{1,0:T(1,128)S(1)}, s32[1,4]{1,0:T(1,128)}, u32[]{:S(2)}) copy-start(s32[1,4]{1,0:T(1,128)} %param.13) | copy-start | bytes 52
  12.2 18.5 %collective-permute-start = (bf16[1,1024,128]{2,1,0:T(8,128)(2,1)S(1)}, bf16[1,1024,128]{2,1,0:T(8,128)(2,1)S(1)}, u32[]{:S(2)}, u32[]{:S(2)}) collective-permute-start(bf16[1,1024,128]{2,1,0:T(8,128)(2,1)S(1)} %get-tuple-element.107), channel_id=1, source_target_pairs={{0,1},{1,0},{2,3},{3,2},{4,5},{5,4},{6,7},{7,6},{8,9},{9,8},{10,11... | collective-permute-start | bytes 786440 | tf_op jit(solution)/shard_map/ppermute | solution.py:30
  14.4 16.3 %collective-permute-start.1 = (bf16[1,1024,128]{2,1,0:T(8,128)(2,1)S(1)}, bf16[1,1024,128]{2,1,0:T(8,128)(2,1)S(1)}, u32[]{:S(2)}, u32[]{:S(2)}) collective-permute-start(bf16[1,1024,128]{2,1,0:T(8,128)(2,1)S(1)} %get-tuple-element.106), channel_id=1, source_target_pairs={{0,2},{1,3},{2,0},{3,1},{4,6},{5,7},{6,4},{7,5},{8,10},{9,11},{10,... | collective-permute-start | bytes 786440 | tf_op jit(solution)/shard_map/ppermute | solution.py:30
  17.0 13.7 %collective-permute-start.2 = (bf16[1,1024,128]{2,1,0:T(8,128)(2,1)S(1)}, bf16[1,1024,128]{2,1,0:T(8,128)(2,1)S(1)}, u32[]{:S(2)}, u32[]{:S(2)}) collective-permute-start(bf16[1,1024,128]{2,1,0:T(8,128)(2,1)S(1)} %get-tuple-element.108), channel_id=1, source_target_pairs={{0,3},{1,2},{2,1},{3,0},{4,7},{5,6},{6,5},{7,4},{8,11},{9,10},{10,... | collective-permute-start | bytes 786440 | tf_op jit(solution)/shard_map/ppermute | solution.py:30
  17.7 12.9 %all-to-all-start = ((s32[4,1,1024]{2,1,0:T(1,128)}), s32[4,1,1024]{2,1,0:T(1,128)S(1)}, u32[]{:S(2)}, u32[]{:S(2)}) async-start(s32[4,1,1024]{2,1,0:T(1,128)} %compare_select_fusion), calls=%async_computation | async-start | bytes 32768 | tf_op jit(solution)/shard_map/all_to_all | solution.py:141
  251.7 2.0 copy-start
  253.7 1.3 copy-start.2
  255.6 3.4 %copy-start.1 = (f32[2,4096,128]{2,1,0:T(8,128)S(1)}, f32[2,4096,128]{2,1,0:T(8,128)}, u32[]{:S(2)}) copy-start(f32[2,4096,128]{2,1,0:T(8,128)} %param.14) | copy-start | bytes 12582916
